TPU v7x, 32 devices: a whole 2x2x4 slice. The times are simulated.
32 devices in a mesh: dp: 4 (over y, core), head: 2 (over x), kv: 4 (over z).
Axes of the slice: x: 2, y: 2, z: 4, core: 2. Of those that a mesh axis runs over, the one named last changes fastest.
Arguments:
- teacher_query: bfloat16 [4, 1024, 3584], P('dp', 'kv', 'head'), may hold values from -96 to 96
- teacher_key: bfloat16 [4, 1024, 512], P('dp', 'kv', 'head'), may hold values from -8 to 8
- student_query: bfloat16 [4, 1024, 1792], P('dp', 'kv', 'head'), may hold values from -96 to 96
- student_key: bfloat16 [4, 1024, 256], P('dp', 'kv', 'head'), may hold values from -8 to 8
- pair_table: int32 [14, 2], replicated, may hold values from 0 to 27, as said below
Outputs:
- kl: float32 [4, 14, 1024], P('dp', 'head', 'kv')
- head_loss: float32 [14], P('head')
Inputs may be any that keep to these rules, and one draw needn't show every extreme that they name: `pair_table`: each of the 28 teacher heads appears exactly once in the table.
All inputs are finite; a program needn't handle non-finite values.
Results may differ from a plain program's by a relative error of at most 0.0003.
Values may be sent and summed in bfloat16 or wider, within the bound.
A program may use at most 64 MiB of HBM per device.

v0:
```python
import math
import jax
import jax.numpy as jnp
from jax import lax
from jax.sharding import PartitionSpec as P

HT = 28
KVT = 4
DH = 128
HS = 14
KVS = 2
masked_value = -1e30


def running_softmax(running_max, running_total, logits, causal_mask):
    filled = jnp.where(causal_mask, logits, masked_value)
    new_max = jnp.maximum(running_max, jnp.max(filled, axis=-1))
    rescale = jnp.exp(running_max - new_max)
    weights = jnp.where(causal_mask, jnp.exp(filled - new_max[..., None]), 0.0)
    return (new_max, running_total * rescale + jnp.sum(weights, axis=-1), rescale, weights)


def make_fold(teacher_heads, teacher_select, student_heads, student_select, repeat, query_pos):
    seq_dev, row_count, pair_count, head_dim = teacher_heads.shape
    student_count = student_heads.shape[2]
    scale = 1.0 / math.sqrt(head_dim)
    last_query = query_pos[row_count - 1]

    def fold_step(carry, pieces, start):
        teacher_keys, student_keys = pieces
        key_count = teacher_keys.shape[1]
        block_size = math.gcd(key_count, 512)
        block_total = key_count // block_size
        visible = jnp.clip(last_query // block_size + 1, 0, block_total)

        def one_block(block_index, state):
            t_max, t_total, t_cross, s_max, s_total = state
            offset = block_index * block_size
            t_block = lax.dynamic_slice_in_dim(teacher_keys, offset, block_size, 1).reshape(
                seq_dev, block_size, -1, head_dim
            )
            s_block = lax.dynamic_slice_in_dim(student_keys, offset, block_size, 1).reshape(
                seq_dev, block_size, -1, head_dim
            )
            t_keys = jnp.take(t_block, teacher_select, axis=2)
            s_keys = jnp.take(s_block, student_select, axis=2)
            t_logits = (
                jnp.einsum(
                    "bqpd,bkpd->bpqk", teacher_heads, t_keys, preferred_element_type=jnp.float32
                )
                * scale
            )
            s_logits = (
                jnp.einsum(
                    "bqsd,bksd->bsqk", student_heads, s_keys, preferred_element_type=jnp.float32
                )
                * scale
            )
            key_pos = offset + jnp.arange(block_size, dtype=jnp.int32)
            causal_mask = key_pos[None, :] <= query_pos[:, None]
            t_max, t_total, t_rescale, t_weights = running_softmax(
                t_max, t_total, t_logits, causal_mask
            )
            s_max, s_total, s_rescale, s_weights = running_softmax(
                s_max, s_total, s_logits, causal_mask
            )
            split_logits = t_logits.reshape(seq_dev, student_count, repeat, row_count, block_size)
            gap = (split_logits - s_logits[:, :, None]).reshape(
                seq_dev, pair_count, row_count, block_size
            )
            t_cross = t_cross * t_rescale + jnp.sum(t_weights * gap, axis=-1)
            return (t_max, t_total, t_cross, s_max, s_total)

        return lax.fori_loop(0, visible, one_block, carry)

    pair_shape = (seq_dev, pair_count, row_count)
    student_shape = (seq_dev, student_count, row_count)
    initial = (
        jnp.full(pair_shape, masked_value, jnp.float32),
        jnp.zeros(pair_shape, jnp.float32),
        jnp.zeros(pair_shape, jnp.float32),
        jnp.full(student_shape, masked_value, jnp.float32),
        jnp.zeros(student_shape, jnp.float32),
    )
    return (fold_step, initial)


def finish_pairs(state, repeat):
    t_max, t_total, t_cross, s_max, s_total = state
    seq_dev, pair_count, row_count = t_max.shape
    student_count = s_max.shape[1]
    t_lse = t_max + jnp.log(t_total)
    s_lse = s_max + jnp.log(s_total)
    s_paired = jnp.broadcast_to(
        s_lse[:, :, None], (seq_dev, student_count, repeat, row_count)
    ).reshape(seq_dev, pair_count, row_count)
    return t_cross / t_total - t_lse + s_paired


def per_device(teacher_query, teacher_key, student_query, student_key, pair_table):
    seq_dev, row_count, teacher_width = teacher_query.shape
    n_head = lax.axis_size("head")
    n_kv = lax.axis_size("kv")
    n_data = lax.axis_size("dp")
    head_index = lax.axis_index("head")
    kv_index = lax.axis_index("kv")
    group_teacher = HT // KVT
    group_student = HS // KVS
    local_student = HS // n_head
    local_student_kv = KVS // n_head
    query_pos = kv_index * row_count + jnp.arange(row_count, dtype=jnp.int32)
    all_tq, all_tk = (
        lax.all_gather(teacher_query, "head", axis=2, tiled=True),
        lax.all_gather(teacher_key, "head", axis=2, tiled=True),
    )
    my_pairs = lax.dynamic_slice_in_dim(
        pair_table, head_index * local_student, local_student, 0
    ).reshape(-1)
    teacher_heads = jnp.take(all_tq.reshape(seq_dev, row_count, HT, DH), my_pairs, axis=2)
    teacher_select = my_pairs // group_teacher
    student_heads = student_query.reshape(seq_dev, row_count, local_student, DH)
    student_ids = head_index * local_student + jnp.arange(local_student, dtype=jnp.int32)
    student_select = student_ids // group_student - head_index * local_student_kv
    fold_step, initial = make_fold(
        teacher_heads, teacher_select, student_heads, student_select, 2, query_pos
    )
    state = fold_step(
        initial,
        (
            lax.all_gather(all_tk, "kv", axis=1, tiled=True),
            lax.all_gather(student_key, "kv", axis=1, tiled=True),
        ),
        jnp.int32(0),
    )
    pair_kl = finish_pairs(state, 2)
    kl_local = jnp.sum(pair_kl.reshape(seq_dev, local_student, 2, row_count), axis=2)
    head_sums = jnp.sum(kl_local, axis=(0, 2))
    total = lax.psum(head_sums, ("dp", "kv"))
    head_loss = total / (seq_dev * n_data * row_count * n_kv)
    return (kl_local, head_loss)


def solution(mesh):
    in_specs = (
        P("dp", "kv", "head"),
        P("dp", "kv", "head"),
        P("dp", "kv", "head"),
        P("dp", "kv", "head"),
        P(),
    )
    out_specs = (P("dp", "head", "kv"), P("head"))
    return jax.shard_map(
        per_device, mesh=mesh, in_specs=in_specs, out_specs=out_specs, check_vma=False
    )
```

profile of v0, /device:TPU:0, one launch (start us, length us, event | category | flops | bytes accessed | tf_op | source)
XLA Modules:
  0.0 131.6 jit_solution(168695083922571773)
XLA Ops:
  7.2 2.3 %copy.18 = bf16[1,256,1792]{1,2,0:T(8,128)(2,1)} copy(bf16[1,256,1792]{2,1,0:T(8,128)(2,1)} %param.7) | data formatting | bytes 1835008 | tf_op args[0]
  9.5 0.0 all-gather.3.cloned.1.call-start
  9.6 1.0 copy.17
  10.6 7.2 %all_gather.12 = bf16[1,256,512]{1,2,0:T(8,128)(2,1)} all-gather(bf16[1,256,256]{1,2,0:T(8,128)(2,1)S(1)} %copy.17), channel_id=1, replica_groups=mesh['dp'=4,'head'=2,'kv'=4] {'head'}, dimensions={2}, use_global_device_ids=true | all-gather | bytes 393216 | tf_op jit(solution)/shard_map/all_gather | solution.py:114
  17.9 0.6 slice.3
  20.1 0.1 constant_dynamic-slice_fusion.1
  20.2 0.1 copy.16
  20.2 0.1 reshape.172
  20.3 0.1 reshape.174
  21.0 0.2 copy.21
  21.2 0.3 copy.22
  21.5 14.4 %all_gather.15 = bf16[1,1024,128]{2,1,0:T(8,128)(2,1)S(1)} all-gather(bf16[1,256,128]{2,1,0:T(8,128)(2,1)S(1)} %copy-done.2), channel_id=1, replica_groups=mesh['dp'=4,'head'=2,'kv'=4] {'kv'}, dimensions={1}, use_global_device_ids=true | all-gather | bytes 327680 | tf_op jit(solution)/shard_map/all_gather | solution.py:131
  35.9 6.6 %all-gather.5.cloned.1.call-done = bf16[1,256,3584]{1,2,0:T(8,128)(2,1)} async-done(((bf16[1,256,1792]{1,2,0:T(8,128)(2,1)}), bf16[1,256,3584]{1,2,0:T(8,128)(2,1)}) %all-gather.5.cloned.1.call-update) | async-done | bytes 1835024 | tf_op jit(solution)/shard_map/all_gather | solution.py:113
  42.5 2.9 %copy.20 = bf16[256,28,128]{2,0,1:T(8,128)(2,1)S(1)} copy(bf16[256,28,128]{0,2,1:T(8,128)(2,1)} %bitcast.99) | data formatting | bytes 3670016 | tf_op jit(solution)/shard_map/reshape | solution.py:119
  45.4 0.7 gather_fusion.1
  46.2 1.1 bitcast_select_fusion.1
  47.3 26.8 %all-gather.3.cloned.1.call-done = bf16[1,1024,512]{1,2,0:T(8,128)(2,1)} async-done(((bf16[1,256,512]{1,2,0:T(8,128)(2,1)}), bf16[1,1024,512]{1,2,0:T(8,128)(2,1)}) %all-gather.3.cloned.1.call-update) | async-done | bytes 1048592 | tf_op jit(solution)/shard_map/all_gather | solution.py:130
  74.1 9.4 %while.19 = (s32[]{:T(128)}, f32[1,14,256]{2,1,0:T(8,128)S(1)}, f32[1,14,256]{2,1,0:T(8,128)S(1)}, f32[1,14,256]{2,1,0:T(8,128)S(1)}, f32[1,7,256]{2,1,0:T(8,128...) while((s32[]{:T(128)}, f32[1,14,256]{2,1,0:T(8,128)S(1)}, ...), condition=%wide.region_6.7_spmd.clone, body=%wide.region_0.6_spmd.clone.sunk | while | flops 732774400 | bytes 36064820 | solution.py:74
  74.1 1.1 constant_dynamic-slice_fusion.3
  75.2 0.3 copy.24
  75.5 0.9 gather_fusion
  76.4 0.1 broadcast_compare_fusion.2
  76.6 2.6 %fusion.28 = (f32[14,256]{1,0:T(8,128)S(1)}, f32[14,512,256]{2,1,0:T(8,128)S(1)}) fusion(pred[256,512]{0,1:T(8,128)(4,1)S(1)} %broadcast_compare_fusion.2, bf16[1,256,14,128]{3,1,2,0:T(8,128)(2,1)} %get-tuple-element.346, bf16[14,512,128]{2,1,0:T(8,128)(2,1)S(1)} %gather_fusion, pred[14]{0:T(512)(128)(4,1)S(1)} %compare_and_fusion.5), kind=kOutput, calls=%fused_computation.9.clone.1 | convolution fusion | flops 476180992 | bytes 10237966 | tf_op jit(solution)/shard_map/while/body/bqpd,bkpd->bpqk/dot_general | solution.py:48
  79.3 0.8 select_reduce_fusion.4
  80.1 2.6 %fusion.29 = (f32[14,256]{1,0:T(8,128)S(1)}, f32[14,256]{1,0:T(8,128)S(1)}) fusion(f32[14,512,256]{2,1,0:T(8,128)S(1)} %get-tuple-element.292, f32[7,256,512]{1,2,0:T(8,128)S(1)} %get-tuple-element.293, f32[14,256]{1,0:T(8,128)S(1)} %bitcast.97, pred[256,512]{0,1:T(8,128)(4,1)S(1)} %broadcast_compare_fusion.2), kind=kLoop, calls=%fused_computation.6.clone.1 | loop fusion | flops 14672896 | bytes 11184128 | tf_op jit(solution)/shard_map/while/body/reduce_sum | solution.py:71
  82.7 0.8 select_reduce_fusion.5
  83.6 0.1 fusion.23
  83.7 0.1 reduce_sum.63
  83.8 0.1 reduce_sum.64
  83.9 0.6 reduce_sum.61
  84.5 39.7 %psum.7 = f32[7]{0:T(128)S(1)} all-reduce(f32[7]{0:T(128)S(1)} %reduce_sum.64), channel_id=1, replica_groups=mesh['dp'=4,'head'=2,'kv'=4] {'dp','kv'}, use_global_device_ids=true, to_apply=%region_10.11 | all-reduce | flops 7 | bytes 56 | tf_op jit(solution)/shard_map/psum | solution.py:138
  124.3 0.5 broadcast_multiply_fusion
  (37 shorter events, 0.3 us)
Async XLA Ops:
  7.2 12.9 %copy-start = (s32[14,2]{0,1:T(2,128)S(1)}, s32[14,2]{0,1:T(2,128)}, u32[]{:S(2)}) copy-start(s32[14,2]{0,1:T(2,128)} %param.11) | copy-start | bytes 340
  7.2 13.8 %copy-start.1 = (bf16[1,256,896]{2,1,0:T(8,128)(2,1)S(1)}, bf16[1,256,896]{2,1,0:T(8,128)(2,1)}, u32[]{:S(2)}) copy-start(bf16[1,256,896]{2,1,0:T(8,128)(2,1)} %param.9) | copy-start | bytes 1376260
  7.2 14.3 %copy-start.2 = (bf16[1,256,128]{2,1,0:T(8,128)(2,1)S(1)}, bf16[1,256,128]{2,1,0:T(8,128)(2,1)}, u32[]{:S(2)}) copy-start(bf16[1,256,128]{2,1,0:T(8,128)(2,1)} %param.10) | copy-start | bytes 196612
  7.2 35.3 %all-gather.5.cloned.1.call-start = ((), (), s32[]{:S(2)}) async-start(), calls=%async_computation.1 | async-start | bytes 2752512 | tf_op jit(solution)/shard_map/all_gather | solution.py:113
  9.5 64.5 %all-gather.3.cloned.1.call-start = ((), (), s32[]{:S(2)}) async-start(), calls=%async_computation | async-start | bytes 1310720 | tf_op jit(solution)/shard_map/all_gather | solution.py:130
Sparse Core Ops, SparseCore 0:
  9.7 32.8 all-gather.4
  44.1 29.9 all-gather.2
where the time goes:
time: 132 us
  blocking collectives  61.4 us (47%)
  waiting for transfers between devices  33.5 us (25%)
  between operations  16.4 us (12%)
  local copies, waits for them, and re-layouts  11.3 us (9%)
  other arithmetic  5.49 us (4%)
  matrix products  3.37 us (3%)
    psum x1, blocking collectives, per_device(): total = lax.psum(head_sums, ('dp', 'kv'))  39.7 us
    all_gather x1, waiting for transfers between devices, per_device(): lax.all_gather(all_tk, 'kv', axis=1, tiled=True)  26.8 us
    all_gather x1, blocking collectives, per_device(): lax.all_gather(student_key, 'kv', axis=1, tiled=True)  14.4 us
    all_gather x1, blocking collectives, per_device(): lax.all_gather(teacher_key, 'head', axis=2, tiled=True)  7.22 us
    all_gather x1, waiting for transfers between devices, per_device(): lax.all_gather(teacher_query, 'head', axis=2, tiled=True)  6.6 us
    unnamed x10, local copies, waits for them, and re-layouts  3.76 us
    reshape x1, local copies, waits for them, and re-layouts, per_device(): all_tq.reshape(seq_dev, row_count, HT, DH)  2.89 us
  transfers between devices with their start and end apart: 2, of which 2 were waited for; matrix products, arithmetic and copies ran while one was open for 5% of the time, Pallas kernels for 0%

commit v1 on v0

--- a/solution.py
+++ b/solution.py
@@ -135,7 +135,7 @@
     pair_kl = finish_pairs(state, 2)
     kl_local = jnp.sum(pair_kl.reshape(seq_dev, local_student, 2, row_count), axis=2)
     head_sums = jnp.sum(kl_local, axis=(0, 2))
-    total = lax.psum(head_sums, ("dp", "kv"))
+    total = jnp.sum(lax.all_gather(head_sums, ("dp", "kv")), axis=0)
     head_loss = total / (seq_dev * n_data * row_count * n_kv)
     return (kl_local, head_loss)
 

time: 132 us -> 132 us (level)
  waiting for transfers between devices: 33.5 us -> 32.1 us
    unnamed x0 -> x1, blocking collectives: none -> 39.7 us
    psum x1 -> x0, blocking collectives: 39.7 us -> none  [per_device(): total = lax.psum(head_sums, ('dp', 'kv'))]
    all_gather x1, waiting for transfers between devices: 6.6 us -> 5.26 us  [per_device(): lax.all_gather(teacher_query, 'head', axis=2, tiled=True)]
    unnamed x10 -> x15, local copies, waits for them, and re-layouts: 3.76 us -> 4.66 us
  transfers between devices with their start and end apart: 2 -> 2, of which waited for: 2 -> 2; matrix products, arithmetic and copies ran while one was open for 5% -> 6% of each run, Pallas kernels for 0% -> 0%
where the time goes in v1:
time: 132 us
  blocking collectives  61.4 us (47%)
  waiting for transfers between devices  32.1 us (24%)
  between operations  17.1 us (13%)
  local copies, waits for them, and re-layouts  12.2 us (9%)
  other arithmetic  5.52 us (4%)
  matrix products  3.37 us (3%)
    unnamed x1, blocking collectives  39.7 us
    all_gather x1, waiting for transfers between devices, per_device(): lax.all_gather(all_tk, 'kv', axis=1, tiled=True)  26.8 us
    all_gather x1, blocking collectives, per_device(): lax.all_gather(student_key, 'kv', axis=1, tiled=True)  14.4 us
    all_gather x1, blocking collectives, per_device(): lax.all_gather(teacher_key, 'head', axis=2, tiled=True)  7.22 us
    all_gather x1, waiting for transfers between devices, per_device(): lax.all_gather(teacher_query, 'head', axis=2, tiled=True)  5.26 us
    unnamed x15, local copies, waits for them, and re-layouts  4.66 us
    reshape x1, local copies, waits for them, and re-layouts, per_device(): all_tq.reshape(seq_dev, row_count, HT, DH)  2.89 us
  transfers between devices with their start and end apart: 2, of which 2 were waited for; matrix products, arithmetic and copies ran while one was open for 6% of the time, Pallas kernels for 0%

profile of v1, /device:TPU:0, one launch (start us, length us, event | category | flops | bytes accessed | tf_op | source)
XLA Modules:
  0.0 132.0 jit_solution(9095631313219517594)
XLA Ops:
  7.3 2.3 %copy.18 = bf16[1,256,1792]{1,2,0:T(8,128)(2,1)} copy(bf16[1,256,1792]{2,1,0:T(8,128)(2,1)} %param.7) | data formatting | bytes 1835008 | tf_op args[0]
  9.6 1.0 copy.17
  10.6 7.2 %all_gather.18 = bf16[1,256,512]{1,2,0:T(8,128)(2,1)} all-gather(bf16[1,256,256]{1,2,0:T(8,128)(2,1)S(1)} %copy.17), channel_id=1, replica_groups=mesh['dp'=4,'head'=2,'kv'=4] {'head'}, dimensions={2}, use_global_device_ids=true | all-gather | bytes 393216 | tf_op jit(solution)/shard_map/all_gather | solution.py:114
  17.9 0.6 slice.3
  20.2 0.1 copy.16
  20.3 0.1 reshape.172
  20.3 0.1 reshape.174
  21.0 0.2 copy.21
  21.2 0.3 copy.22
  21.5 0.6 dynamic-slice
  22.9 14.4 %all_gather.21 = bf16[1,1024,128]{2,1,0:T(8,128)(2,1)S(1)} all-gather(bf16[1,256,128]{2,1,0:T(8,128)(2,1)S(1)} %copy-done.2), channel_id=1, replica_groups=mesh['dp'=4,'head'=2,'kv'=4] {'kv'}, dimensions={1}, use_global_device_ids=true | all-gather | bytes 327680 | tf_op jit(solution)/shard_map/all_gather | solution.py:131
  37.3 5.3 %all-gather.6.cloned.1.call-done = bf16[1,256,3584]{1,2,0:T(8,128)(2,1)} async-done(((bf16[1,256,1792]{1,2,0:T(8,128)(2,1)}), bf16[1,256,3584]{1,2,0:T(8,128)(2,1)}) %all-gather.6.cloned.1.call-update) | async-done | bytes 1835024 | tf_op jit(solution)/shard_map/all_gather | solution.py:113
  42.6 2.9 %copy.20 = bf16[256,28,128]{2,0,1:T(8,128)(2,1)S(1)} copy(bf16[256,28,128]{0,2,1:T(8,128)(2,1)} %bitcast.100) | data formatting | bytes 3670016 | tf_op jit(solution)/shard_map/reshape | solution.py:119
  45.5 0.7 gather_fusion.1
  46.2 1.1 bitcast_select_fusion.1
  47.3 26.8 %all-gather.4.cloned.1.call-done = bf16[1,1024,512]{1,2,0:T(8,128)(2,1)} async-done(((bf16[1,256,512]{1,2,0:T(8,128)(2,1)}), bf16[1,1024,512]{1,2,0:T(8,128)(2,1)}) %all-gather.4.cloned.1.call-update) | async-done | bytes 1048592 | tf_op jit(solution)/shard_map/all_gather | solution.py:130
  74.1 9.4 %while.19 = (s32[]{:T(128)}, f32[1,14,256]{2,1,0:T(8,128)S(1)}, f32[1,14,256]{2,1,0:T(8,128)S(1)}, f32[1,14,256]{2,1,0:T(8,128)S(1)}, f32[1,7,256]{2,1,0:T(8,128...) while((s32[]{:T(128)}, f32[1,14,256]{2,1,0:T(8,128)S(1)}, ...), condition=%wide.region_6.7_spmd.clone, body=%wide.region_0.6_spmd.clone.sunk | while | flops 732774400 | bytes 36064820 | solution.py:74
  74.1 1.1 constant_dynamic-slice_fusion.3
  75.2 0.3 copy.24
  75.5 0.9 gather_fusion
  76.5 0.1 broadcast_compare_fusion.2
  76.6 2.6 %fusion.28 = (f32[14,256]{1,0:T(8,128)S(1)}, f32[14,512,256]{2,1,0:T(8,128)S(1)}) fusion(pred[256,512]{0,1:T(8,128)(4,1)S(1)} %broadcast_compare_fusion.2, bf16[1,256,14,128]{3,1,2,0:T(8,128)(2,1)} %get-tuple-element.346, bf16[14,512,128]{2,1,0:T(8,128)(2,1)S(1)} %gather_fusion, pred[14]{0:T(512)(128)(4,1)S(1)} %compare_and_fusion.5), kind=kOutput, calls=%fused_computation.9.clone.1 | convolution fusion | flops 476180992 | bytes 10237966 | tf_op jit(solution)/shard_map/while/body/bqpd,bkpd->bpqk/dot_general | solution.py:48
  79.3 0.8 select_reduce_fusion.4
  80.1 2.6 %fusion.29 = (f32[14,256]{1,0:T(8,128)S(1)}, f32[14,256]{1,0:T(8,128)S(1)}) fusion(f32[14,512,256]{2,1,0:T(8,128)S(1)} %get-tuple-element.292, f32[7,256,512]{1,2,0:T(8,128)S(1)} %get-tuple-element.293, f32[14,256]{1,0:T(8,128)S(1)} %bitcast.98, pred[256,512]{0,1:T(8,128)(4,1)S(1)} %broadcast_compare_fusion.2), kind=kLoop, calls=%fused_computation.6.clone.1 | loop fusion | flops 14672896 | bytes 11184128 | tf_op jit(solution)/shard_map/while/body/reduce_sum | solution.py:71
  82.7 0.8 select_reduce_fusion.5
  83.6 0.1 fusion.23
  83.7 0.6 reduce_sum.70
  84.4 0.1 reduce_sum.73
  84.5 0.2 dynamic-update-slice
  84.8 39.7 %all-reduce = f32[112]{0:T(128)S(1)} all-reduce(f32[112]{0:T(128)S(1)} %dynamic-update-slice), channel_id=2, replica_groups=mesh['dp'=4,'head'=2,'kv'=4] {'dp','kv'}, use_global_device_ids=true, to_apply=%add | all-reduce | flops 112 | bytes 896
  124.5 0.1 reshape.200
  124.6 0.5 broadcast_multiply_fusion
  (44 shorter events, 0.5 us)
Async XLA Ops:
  7.2 12.9 %copy-start = (s32[14,2]{0,1:T(2,128)S(1)}, s32[14,2]{0,1:T(2,128)}, u32[]{:S(2)}) copy-start(s32[14,2]{0,1:T(2,128)} %param.11) | copy-start | bytes 340
  7.2 14.3 %copy-start.3 = (u32[32]{0:T(128)S(1)}, u32[32]{0:T(128)}, u32[]{:S(2)}) copy-start(u32[32]{0:T(128)} %constant.119) | copy-start | bytes 388
  7.2 13.8 %copy-start.1 = (bf16[1,256,896]{2,1,0:T(8,128)(2,1)S(1)}, bf16[1,256,896]{2,1,0:T(8,128)(2,1)}, u32[]{:S(2)}) copy-start(bf16[1,256,896]{2,1,0:T(8,128)(2,1)} %param.9) | copy-start | bytes 1376260
  7.2 15.6 %copy-start.2 = (bf16[1,256,128]{2,1,0:T(8,128)(2,1)S(1)}, bf16[1,256,128]{2,1,0:T(8,128)(2,1)}, u32[]{:S(2)}) copy-start(bf16[1,256,128]{2,1,0:T(8,128)(2,1)} %param.10) | copy-start | bytes 196612
  7.2 35.3 %all-gather.6.cloned.1.call-start = ((), (), s32[]{:S(2)}) async-start(), calls=%async_computation.1 | async-start | bytes 2752512 | tf_op jit(solution)/shard_map/all_gather | solution.py:113
  9.5 64.5 %all-gather.4.cloned.1.call-start = ((), (), s32[]{:S(2)}) async-start(), calls=%async_computation | async-start | bytes 1310720 | tf_op jit(solution)/shard_map/all_gather | solution.py:130
Sparse Core Ops, SparseCore 0:
  9.7 32.8 all-gather.5
  44.1 29.9 all-gather.3
